TPU v7x, 32 devices: a whole 2x2x4 slice. The times are simulated.
32 devices in a mesh: dp: 8 (over z, y), mp: 4 (over x, core).
Axes of the slice: x: 2, y: 2, z: 4, core: 2. Of those that a mesh axis runs over, the one named last changes fastest.
Arguments:
- tokens: bfloat16 [12288, 768], P('dp'), may hold values from -6 to 6
- segment_ids: int32 [12288], P('dp'), may hold values from 0 to 47, as said below
- first_gain: bfloat16 [768], replicated, may hold values from 0.25 to 1.75
- first_shift: bfloat16 [768], replicated, may hold values from -3 to 3
- qkv_weight: bfloat16 [768, 3, 768], P(None, None, 'mp'), may hold values from -0.21875 to 0.21875
- qv_bias: bfloat16 [2, 12, 64], P(None, 'mp'), may hold values from -3 to 3
- proj_weight: bfloat16 [768, 768], P('mp'), may hold values from -1.25 to 1.25
- proj_bias: bfloat16 [768], replicated, may hold values from -3 to 3
- second_gain: bfloat16 [768], replicated, may hold values from 0.25 to 1.75
- second_shift: bfloat16 [768], replicated, may hold values from -3 to 3
- up_weight: bfloat16 [768, 3072], P(None, 'mp'), may hold values from -0.21875 to 0.21875
- up_bias: bfloat16 [48, 64], P('mp'), may hold values from -3 to 3
- down_weight: bfloat16 [3072, 768], P('mp'), may hold values from -0.109375 to 0.109375
- down_bias: bfloat16 [768], replicated, may hold values from -3 to 3
- cotangent: bfloat16 [12288, 768], P('dp'), may hold values from -6 to 6
Outputs:
- layer_output: bfloat16 [12288, 768], P('dp')
- input_grad: bfloat16 [12288, 768], P('dp')
- first_gain_grad: float32 [768], P('dp')
- first_shift_grad: float32 [768], P('dp')
- qkv_weight_grad: float32 [768, 3, 768], P('dp', None, 'mp')
- qv_bias_grad: float32 [2, 12, 64], P(None, 'mp', 'dp')
- proj_weight_grad: float32 [768, 768], P('mp', 'dp')
- proj_bias_grad: float32 [768], P('dp')
- second_gain_grad: float32 [768], P('dp')
- second_shift_grad: float32 [768], P('dp')
- up_weight_grad: float32 [768, 3072], P('dp', 'mp')
- up_bias_grad: float32 [48, 64], P('mp', 'dp')
- down_weight_grad: float32 [3072, 768], P('mp', 'dp')
- down_bias_grad: float32 [768], P('dp')
Inputs may be any that keep to these rules, and one draw needn't show every extreme that they name: `segment_ids`: in each sequence of 512 tokens the first 16 * r tokens carry one even id and the others that id plus one, with r from 8 to 24; different sequences have different ids.
All inputs are finite; a program needn't handle non-finite values.
Results may differ from a plain program's by a relative error of at most 0.013.
Values sent between devices are 32-bit elements; how exact they have to be, the bound alone decides.
A program may use at most 128 MiB of HBM per device.

v0:
```python
import jax
import jax.numpy as jnp
from jax import lax
from jax.sharding import PartitionSpec as P

LEN = 512
EPS = 1e-06
SCALE = 0.125
NEGATIVE = -1e30


def normalize(values):
    centre = values - jnp.mean(values, axis=-1, keepdims=True)
    inverse = lax.rsqrt(jnp.mean(centre * centre, axis=-1, keepdims=True) + EPS)
    return (centre * inverse, inverse)


def norm_backward(grad_normed, unit, inverse, gain):
    scaled = grad_normed * gain
    return inverse * (
        scaled
        - jnp.mean(scaled, axis=-1, keepdims=True)
        - unit * jnp.mean(scaled * unit, axis=-1, keepdims=True)
    )


def exact_gelu(values):
    return jax.nn.gelu(values, approximate=False)


def masked_scores(query, keys, labels):
    raw = jnp.einsum("qhe,khe->hqk", query, keys, preferred_element_type=jnp.float32)
    same = labels[:, None] == labels[None, :]
    return jnp.where(same[None], SCALE * raw, NEGATIVE)


def attend(items):
    triple, labels = items
    scores = masked_scores(triple[:, 0], triple[:, 1], labels)
    top = jnp.max(scores, axis=-1, keepdims=True)
    expo = jnp.exp(scores - top)
    total = jnp.sum(expo, axis=-1, keepdims=True)
    probs = expo / total
    mixed = jnp.einsum(
        "hqk,khe->qhe", probs.astype(jnp.bfloat16), triple[:, 2], preferred_element_type=jnp.float32
    )
    return (mixed.astype(jnp.bfloat16), top + jnp.log(total))


def attend_back(items):
    triple, labels, grad_mixed, log_total = items
    query = triple[:, 0]
    keys = triple[:, 1]
    values = triple[:, 2]
    probs = jnp.exp(masked_scores(query, keys, labels) - log_total)
    grad_probs = jnp.einsum("qhe,khe->hqk", grad_mixed, values, preferred_element_type=jnp.float32)
    inner = jnp.sum(probs * grad_probs, axis=-1, keepdims=True)
    grad_scores = (probs * (grad_probs - inner)).astype(jnp.bfloat16)
    grad_query = SCALE * jnp.einsum(
        "hqk,khe->qhe", grad_scores, keys, preferred_element_type=jnp.float32
    )
    grad_keys = SCALE * jnp.einsum(
        "hqk,qhe->khe", grad_scores, query, preferred_element_type=jnp.float32
    )
    grad_values = jnp.einsum(
        "hqk,qhe->khe", probs.astype(jnp.bfloat16), grad_mixed, preferred_element_type=jnp.float32
    )
    return jnp.stack([grad_query, grad_keys, grad_values], axis=1).astype(jnp.bfloat16)


def shards(
    tokens,
    segment_ids,
    first_gain,
    first_shift,
    qkv_weight,
    qv_bias,
    proj_weight,
    proj_bias,
    second_gain,
    second_shift,
    up_weight,
    up_bias,
    down_weight,
    down_bias,
    cotangent,
):
    rows = tokens.shape[0]
    heads_here = qv_bias.shape[1]
    head_size = qv_bias.shape[2]
    local_width = heads_here * head_size
    count = rows // LEN
    gain_one = first_gain.astype(jnp.float32)
    gain_two = second_gain.astype(jnp.float32)
    inputs = tokens.astype(jnp.float32)
    first_unit, first_inverse = normalize(inputs)
    normed1 = (first_unit * gain_one + first_shift.astype(jnp.float32)).astype(jnp.bfloat16)
    projected = jnp.einsum("nd,dce->nce", normed1, qkv_weight, preferred_element_type=jnp.float32)
    query_bias = qv_bias[0].reshape(local_width).astype(jnp.float32)
    bias_rows = jnp.stack(
        [
            query_bias,
            jnp.zeros_like(query_bias),
            qv_bias[1].reshape(local_width).astype(jnp.float32),
        ]
    )
    triple = (
        (projected + bias_rows).astype(jnp.bfloat16).reshape(count, LEN, 3, heads_here, head_size)
    )
    image_ids = segment_ids.reshape(count, LEN)
    mixed, log_total = lax.map(attend, (triple, image_ids))
    mixed_rows = mixed.reshape(rows, local_width)
    head_part = jnp.dot(mixed_rows, proj_weight, preferred_element_type=jnp.float32)
    attended = lax.psum(head_part, "mp")
    middle = inputs + attended + proj_bias.astype(jnp.float32)
    second_unit, second_inverse = normalize(middle)
    normed2 = (second_unit * gain_two + second_shift.astype(jnp.float32)).astype(jnp.bfloat16)
    up_flat = up_bias.reshape(-1).astype(jnp.float32)
    hidden_pre = jnp.dot(normed2, up_weight, preferred_element_type=jnp.float32) + up_flat
    activated, gelu_pull = jax.vjp(exact_gelu, hidden_pre)
    hidden = activated.astype(jnp.bfloat16)
    column_part = jnp.dot(hidden, down_weight, preferred_element_type=jnp.float32)
    fed = lax.psum(column_part, "mp")
    layer_output = (middle + fed + down_bias.astype(jnp.float32)).astype(jnp.bfloat16)
    grad_out = cotangent.astype(jnp.float32)
    down_bias_grad = jnp.sum(grad_out, axis=0)
    down_weight_grad = jnp.einsum(
        "nf,nd->fd", hidden, cotangent, preferred_element_type=jnp.float32
    )
    grad_hidden = jnp.einsum(
        "nd,fd->nf", cotangent, down_weight, preferred_element_type=jnp.float32
    )
    normed_again = lax.optimization_barrier(normed2)
    pre_again = jnp.dot(normed_again, up_weight, preferred_element_type=jnp.float32) + up_flat
    unused, pull_again = jax.vjp(exact_gelu, pre_again)
    grad_pre = pull_again(grad_hidden)[0]
    grad_pre_low = grad_pre.astype(jnp.bfloat16)
    up_bias_grad = jnp.sum(grad_pre_low, axis=0, dtype=jnp.float32).reshape(up_bias.shape)
    up_weight_grad = jnp.einsum(
        "nd,nf->df", normed2, grad_pre_low, preferred_element_type=jnp.float32
    )
    column_back_part = jnp.einsum(
        "nf,df->nd", grad_pre_low, up_weight, preferred_element_type=jnp.float32
    )
    grad_normed2 = lax.psum(column_back_part, "mp")
    second_gain_grad = jnp.sum(grad_normed2 * second_unit, axis=0)
    second_shift_grad = jnp.sum(grad_normed2, axis=0)
    grad_middle = grad_out + norm_backward(grad_normed2, second_unit, second_inverse, gain_two)
    proj_bias_grad = jnp.sum(grad_middle, axis=0)
    middle_low = grad_middle.astype(jnp.bfloat16)
    proj_weight_grad = jnp.einsum(
        "ne,nd->ed", mixed_rows, middle_low, preferred_element_type=jnp.float32
    )
    grad_mixed = jnp.einsum(
        "nd,ed->ne", middle_low, proj_weight, preferred_element_type=jnp.float32
    )
    grad_mixed = grad_mixed.astype(jnp.bfloat16).reshape(count, LEN, heads_here, head_size)
    grad_triple = lax.map(attend_back, (triple, image_ids, grad_mixed, log_total))
    grad_rows = grad_triple.reshape(rows, 3, local_width)
    qv_bias_grad = jnp.stack(
        [
            jnp.sum(grad_rows[:, 0], axis=0, dtype=jnp.float32),
            jnp.sum(grad_rows[:, 2], axis=0, dtype=jnp.float32),
        ]
    ).reshape(2, heads_here, head_size)
    qkv_weight_grad = jnp.einsum(
        "nd,nce->dce", normed1, grad_rows, preferred_element_type=jnp.float32
    )
    head_back_part = jnp.einsum(
        "nce,dce->nd", grad_rows, qkv_weight, preferred_element_type=jnp.float32
    )
    grad_normed1 = lax.psum(head_back_part, "mp")
    first_gain_grad = jnp.sum(grad_normed1 * first_unit, axis=0)
    first_shift_grad = jnp.sum(grad_normed1, axis=0)
    input_grad = (
        grad_middle + norm_backward(grad_normed1, first_unit, first_inverse, gain_one)
    ).astype(jnp.bfloat16)
    summed = (
        lax.psum_scatter(qkv_weight_grad, "dp", scatter_dimension=0, tiled=True),
        lax.psum_scatter(qv_bias_grad, "dp", scatter_dimension=2, tiled=True),
        lax.psum_scatter(proj_weight_grad, "dp", scatter_dimension=1, tiled=True),
        lax.psum_scatter(proj_bias_grad, "dp", scatter_dimension=0, tiled=True),
        lax.psum_scatter(first_gain_grad, "dp", scatter_dimension=0, tiled=True),
        lax.psum_scatter(first_shift_grad, "dp", scatter_dimension=0, tiled=True),
        lax.psum_scatter(down_weight_grad, "dp", scatter_dimension=1, tiled=True),
        lax.psum_scatter(down_bias_grad, "dp", scatter_dimension=0, tiled=True),
        lax.psum_scatter(up_weight_grad, "dp", scatter_dimension=0, tiled=True),
        lax.psum_scatter(up_bias_grad, "dp", scatter_dimension=1, tiled=True),
        lax.psum_scatter(second_gain_grad, "dp", scatter_dimension=0, tiled=True),
        lax.psum_scatter(second_shift_grad, "dp", scatter_dimension=0, tiled=True),
    )
    head_sums = summed[:6]
    column_sums = summed[6:]
    return (
        layer_output,
        input_grad,
        head_sums[4],
        head_sums[5],
        head_sums[0],
        head_sums[1],
        head_sums[2],
        head_sums[3],
        column_sums[4],
        column_sums[5],
        column_sums[2],
        column_sums[3],
        column_sums[0],
        column_sums[1],
    )


def solution(mesh):
    in_specs = (
        P("dp", None),
        P("dp"),
        P(),
        P(),
        P(None, None, "mp"),
        P(None, "mp", None),
        P("mp", None),
        P(),
        P(),
        P(),
        P(None, "mp"),
        P("mp", None),
        P("mp", None),
        P(),
        P("dp", None),
    )
    out_specs = (
        P("dp", None),
        P("dp", None),
        P("dp"),
        P("dp"),
        P("dp", None, "mp"),
        P(None, "mp", "dp"),
        P("mp", "dp"),
        P("dp"),
        P("dp"),
        P("dp"),
        P("dp", "mp"),
        P("mp", "dp"),
        P("mp", "dp"),
        P("dp"),
    )
    return jax.shard_map(shards, mesh=mesh, in_specs=in_specs, out_specs=out_specs, check_vma=False)
```

profile of v0, /device:TPU:0, one launch (start us, length us, event | category | flops | bytes accessed | tf_op | source)
XLA Modules:
  0.0 749.1 jit_solution(18400123247982179600)
XLA Ops:
  13.8 2.5 fusion.42
  19.8 5.2 reshape.266
  24.9 3.4 copy.53
  28.3 15.6 %while.22 = (s32[]{:T(128)}, bf16[3,512,3,64]{1,3,2,0:T(8,128)(2,1)}, f32[3,3,512,1]{2,1,3,0:T(4,128)}, bf16[3,512,3,3,64]{1,4,3,2,0:T(8,128)(2,1)}, s32[3,512]{1,0:T(4,128)S(1)}, /*index=5*/s32[]{:T(128)}) while((s32[]{:T(128)}, bf16[3,512,3,64]{1,3,2,0:T(8,128)(2,1)}, f32[3,3,512,1]{2,1,3,0:T(4,128)}, bf16[3,512,3,3,64]{1,4,3,2,0:T(8,128)(2,1)}, ...), condition=%wide.region_5.6_spmd, body=%wide.region_2.5_spmd.sunk | while | flops 211122688 | bytes 12513373 | solution.py:111
  46.5 4.0 fusion.76
  53.7 6.4 fusion.78
  60.1 87.3 %all-reduce.14.cloned.1.call-done = f32[1536,768]{1,0:T(8,128)} async-done(((f32[1536,768]{1,0:T(8,128)}), f32[1536,768]{1,0:T(8,128)}) %all-reduce.14.cloned.1.call-update) | async-done | bytes 4718608 | tf_op jit(solution)/shard_map/psum | solution.py:114
  147.4 3.1 fusion.74
  154.4 14.3 %convert_reduce_fusion.2 = (f32[768]{0:T(1024)}, bf16[1536,768]{1,0:T(8,128)(2,1)S(1)}) fusion(f32[1536,768]{1,0:T(8,128)S(1)} %bitcast.167, f32[768]{0:T(1024)S(1)} %copy-done.37, bf16[1536,768]{1,0:T(8,128)(2,1)S(1)} %add_convert_fusion.1, bf16[768,768]{1,0:T(8,128)(2,1)S(1)} %copy-done), kind=kOutput, calls=%fused_computation.78 | convolution fusion | flops 1900412160 | bytes 10622976 | tf_op jit(solution)/shard_map/dot_general | solution.py:134
  170.1 4.2 fusion.79
  175.0 12.9 %fusion.46 = bf16[1536,768]{1,0:T(8,128)(2,1)S(1)} fusion(bf16[1536,768]{1,0:T(8,128)(2,1)S(1)} %add_convert_fusion.1, bf16[768,768]{1,0:T(8,128)(2,1)S(1)} %copy-done, f32[768]{0:T(1024)} %reshape.274), kind=kOutput, calls=%fused_computation.72 | convolution fusion | flops 1889796096 | bytes 5901312 | tf_op jit(solution)/shard_map/dot_general | solution.py:119
  189.4 4.3 fusion.77
  193.7 75.0 %all-reduce.16.cloned.1.call-done = f32[1536,768]{1,0:T(8,128)} async-done(((f32[1536,768]{1,0:T(8,128)}), f32[1536,768]{1,0:T(8,128)}) %all-reduce.16.cloned.1.call-update) | async-done | bytes 4718608 | tf_op jit(solution)/shard_map/psum | solution.py:145
  268.7 5.6 multiply_reduce_fusion.1
  274.3 4.9 fusion.73
  283.4 3.4 convolution_convert_fusion
  287.6 21.1 %while.23 = (s32[]{:T(128)}, bf16[3,512,3,3,64]{1,4,3,2,0:T(8,128)(2,1)S(1)}, bf16[3,512,3,3,64]{1,4,3,2,0:T(8,128)(2,1)}, s32[3,512]{1,0:T(4,128)}, f32[3,3,512...) while((s32[]{:T(128)}, bf16[3,512,3,3,64]{1,4,3,2,0:T(8,128)(2,1)S(1)}, ...), condition=%wide.region_15.16_spmd, body=%wide.region_13.15_spmd.sunk | while | flops 512915968 | bytes 28481644 | solution.py:158
  309.9 3.1 copy.57
  313.0 3.8 reshape.270
  316.8 5.8 convolution_bitcast_fusion
  324.2 5.1 fusion.81
  329.7 6.1 fusion.80
  336.0 5.4 fusion.66
  345.1 5.3 reduce-scatter.15.cloned.1.call-done
  352.1 169.7 %all-reduce.18.cloned.1.call-done = (f32[1536,768]{1,0:T(8,128)}, f32[1536,768]{1,0:T(8,128)}) async-done(((f32[1536,768]{1,0:T(8,128)}, f32[1536,768]{1,0:T(8,128)}), (f32[1536,768]{1,0:T(8,128)}, f32[1536,768]{1,0:T(8,128)})) %all-reduce.18.cloned.1.call-update) | async-done | bytes 9437200 | tf_op jit(solution)/shard_map/psum | solution.py:123
  521.8 4.3 fusion.41
  526.2 37.9 %all-reduce.8 = (f32[768]{0:T(1024)S(1)}, f32[768]{0:T(1024)S(1)}, f32[2,3,64]{2,1,0:T(4,128)S(1)}, f32[768]{0:T(1024)S(1)}, f32[768]{0:T(1024)S(1)}, /*index=5*...) all-reduce(f32[768]{0:T(1024)S(1)} %get-tuple-element.140, ...), channel_id=2, replica_groups=mesh['dp'=8,'mp'=4] {'dp'}, use_global_device_ids=true, to_apply=%region_20.21.clone | all-reduce | flops 5760 | bytes 46080
  569.0 6.0 add_convert_fusion
  576.9 2.8 fusion.40
  579.8 16.4 %reduce-scatter.13.cloned.1.call-done = f32[768,96]{0,1:T(8,128)} async-done(((f32[768,768]{0,1:T(8,128)}), f32[768,96]{0,1:T(8,128)}) %reduce-scatter.13.cloned.1.call-update) | async-done | bytes 294928 | tf_op jit(solution)/shard_map/reduce_scatter | solution.py:185
  596.2 72.9 %reduce-scatter.11.cloned.1.call-done = f32[96,768]{1,0:T(8,128)} async-done(((f32[768,768]{1,0:T(8,128)}), f32[96,768]{1,0:T(8,128)}) %reduce-scatter.11.cloned.1.call-update) | async-done | bytes 294928 | tf_op jit(solution)/shard_map/reduce_scatter | solution.py:187
  669.0 72.9 %reduce-scatter.9.cloned.1.call-done = f32[96,3,192]{2,0,1:T(8,128)} async-done(((f32[768,3,192]{2,0,1:T(8,128)}), f32[96,3,192]{2,0,1:T(8,128)}) %reduce-scatter.9.cloned.1.call-update) | async-done | bytes 221200 | tf_op jit(solution)/shard_map/reduce_scatter | solution.py:179
  (224 shorter events, 78.5 us)
Async XLA Ops:
  7.2 145.7 %copy-start = (bf16[768,768]{1,0:T(8,128)(2,1)S(1)}, bf16[768,768]{1,0:T(8,128)(2,1)}, u32[]{:S(2)}) copy-start(bf16[768,768]{1,0:T(8,128)(2,1)} %param.29) | copy-start | bytes 3538948
  7.2 9.3 %copy-start.4 = (bf16[1536,768]{1,0:T(8,128)(2,1)S(1)}, bf16[1536,768]{1,0:T(8,128)(2,1)}, u32[]{:S(2)}) copy-start(bf16[1536,768]{1,0:T(8,128)(2,1)} %param.19) | copy-start | bytes 7077892
  7.2 140.2 %all-reduce.14.cloned.1.call-start = ((), (), s32[]{:S(2)}) async-start(), calls=%async_computation.4 | async-start | bytes 9437184 | tf_op jit(solution)/shard_map/psum | solution.py:114
  8.1 10.2 %copy-start.25 = (f32[768]{0:T(1024)}, f32[768]{0:T(1024)S(1)}, u32[]{:S(2)}) copy-start(f32[768]{0:T(1024)S(1)} %convert_element_type.122) | copy-start | bytes 9220
  8.9 9.4 %copy-start.34 = (f32[768]{0:T(1024)}, f32[768]{0:T(1024)S(1)}, u32[]{:S(2)}) copy-start(f32[768]{0:T(1024)S(1)} %convert_element_type.123) | copy-start | bytes 9220
  50.5 218.2 %all-reduce.16.cloned.1.call-start = ((), (), s32[]{:S(2)}) async-start(), calls=%async_computation.5 | async-start | bytes 9437184 | tf_op jit(solution)/shard_map/psum | solution.py:145
  154.4 20.6 %copy-start.9 = (bf16[1536,768]{1,0:T(8,128)(2,1)}, bf16[1536,768]{1,0:T(8,128)(2,1)S(1)}, u32[]{:S(2)}) copy-start(bf16[1536,768]{1,0:T(8,128)(2,1)S(1)} %add_convert_fusion.1) | copy-start | bytes 7077892
  174.4 176.1 %reduce-scatter.15.cloned.1.call-start = ((), (), s32[]{:S(2)}) async-start(), calls=%async_computation.9 | async-start | bytes 884736
  175.0 14.5 %copy-start.43 = (bf16[768,768]{1,0:T(8,128)(2,1)S(1)}, bf16[768,768]{1,0:T(8,128)(2,1)}, u32[]{:S(2)}) copy-start(bf16[768,768]{1,0:T(8,128)(2,1)} %param.31) | copy-start | bytes 3538948
  189.4 79.3 %copy-start.24 = (f32[768]{0:T(1024)S(1)}, f32[768]{0:T(1024)}, u32[]{:S(2)}) copy-start(f32[768]{0:T(1024)} %convert_element_type.131) | copy-start | bytes 9220
  193.7 80.6 %copy-start.13 = (bf16[1536,768]{1,0:T(8,128)(2,1)S(1)}, bf16[1536,768]{1,0:T(8,128)(2,1)}, u32[]{:S(2)}) copy-start(bf16[1536,768]{1,0:T(8,128)(2,1)} %param.33) | copy-start | bytes 7077892
  274.3 7.1 copy-start.11
  286.8 235.0 %all-reduce.18.cloned.1.call-start = ((), (), s32[]{:S(2)}) async-start(), calls=%async_computation.10 | async-start | bytes 18874368 | tf_op jit(solution)/shard_map/psum | solution.py:123
  309.9 6.9 copy-start.45
  322.6 273.6 %reduce-scatter.13.cloned.1.call-start = ((), (), s32[]{:S(2)}) async-start(), calls=%async_computation.8 | async-start | bytes 2654208 | tf_op jit(solution)/shard_map/reduce_scatter | solution.py:185
  329.4 6.6 copy-start.5
  329.4 6.6 copy-start.19
  329.4 6.6 copy-start.22
  329.4 6.6 copy-start.26
  329.4 6.6 copy-start.35
  329.4 339.6 %reduce-scatter.11.cloned.1.call-start = ((), (), s32[]{:S(2)}) async-start(), calls=%async_computation.7 | async-start | bytes 2654208 | tf_op jit(solution)/shard_map/reduce_scatter | solution.py:187
  335.9 7.5 %copy-start.42 = (bf16[768]{0:T(1024)(128)(2,1)S(1)}, bf16[768]{0:T(1024)(128)(2,1)}, u32[]{:S(2)}) copy-start(bf16[768]{0:T(1024)(128)(2,1)} %param.32) | copy-start | bytes 4612
  335.9 7.5 %copy-start.33 = (f32[768]{0:T(1024)S(1)}, f32[768]{0:T(1024)}, u32[]{:S(2)}) copy-start(f32[768]{0:T(1024)} %get-tuple-element.191) | copy-start | bytes 9220
  335.9 406.1 %reduce-scatter.9.cloned.1.call-start = ((), (), s32[]{:S(2)}) async-start(), calls=%async_computation.6 | async-start | bytes 2654208 | tf_op jit(solution)/shard_map/reduce_scatter | solution.py:179
  341.5 184.7 %copy-start.28 = (f32[768]{0:T(1024)S(1)}, f32[768]{0:T(1024)}, u32[]{:S(2)}) copy-start(f32[768]{0:T(1024)} %get-tuple-element.138) | copy-start | bytes 9220
  341.5 184.7 %copy-start.29 = (f32[768]{0:T(1024)S(1)}, f32[768]{0:T(1024)}, u32[]{:S(2)}) copy-start(f32[768]{0:T(1024)} %get-tuple-element.144) | copy-start | bytes 9220
  341.5 184.7 %copy-start.31 = (f32[768]{0:T(1024)S(1)}, f32[768]{0:T(1024)}, u32[]{:S(2)}) copy-start(f32[768]{0:T(1024)} %get-tuple-element.182) | copy-start | bytes 9220
  341.5 184.7 %copy-start.32 = (f32[768]{0:T(1024)S(1)}, f32[768]{0:T(1024)}, u32[]{:S(2)}) copy-start(f32[768]{0:T(1024)} %get-tuple-element.190) | copy-start | bytes 9220
  521.8 53.2 %slice-start = ((s8[4718592]{0:T(1024)(128)(4,1)}), s8[524288]{0:T(1024)(128)(4,1)S(1)}, s32[]{:S(2)}) async-start(s8[4718592]{0:T(1024)(128)(4,1)} %bitcast.156), calls=%async_computation.11 | async-start | bytes 1048576
  568.9 8.0 %copy-start.8 = (f32[1536,768]{1,0:T(8,128)S(1)}, f32[1536,768]{1,0:T(8,128)}, u32[]{:S(2)}) copy-start(f32[1536,768]{1,0:T(8,128)} %get-tuple-element.181) | copy-start | bytes 14155780
  569.0 8.0 %copy-start.27 = (f32[768]{0:T(1024)S(1)}, f32[768]{0:T(1024)}, u32[]{:S(2)}) copy-start(f32[768]{0:T(1024)} %copy-done.25) | copy-start | bytes 9220
  569.0 173.0 %copy-start.1 = (bf16[768,768]{1,0:T(8,128)(2,1)S(1)}, bf16[768,768]{1,0:T(8,128)(2,1)}, u32[]{:S(2)}) copy-start(bf16[768,768]{1,0:T(8,128)(2,1)} %param.29) | copy-start | bytes 3538948
  (27 other events, 88.4 us)
Sparse Core Ops, SparseCore 0:
  50.6 96.7 all-reduce.13
  174.5 94.1 all-reduce.15
  286.9 63.5 reduce-scatter.14
  352.9 168.8 all-reduce.17
  525.7 70.4 reduce-scatter.12
  600.1 68.9 reduce-scatter.10
  673.1 68.8 reduce-scatter.8
where the time goes:
time: 756 us; the launch traced here: 749 us
  waiting for transfers between devices  500 us (66%)
  matrix products  93.4 us (12%)
  local copies, waits for them, and re-layouts  51.9 us (7%)
  other arithmetic  48.3 us (6%)
  blocking collectives  37.9 us (5%)
  between operations  16.3 us (2%)
    psum x1, waiting for transfers between devices, shards(): fed = lax.psum(column_part, 'mp')  170 us
    psum x1, waiting for transfers between devices, shards(): attended = lax.psum(head_part, 'mp')  87.3 us
    psum x1, waiting for transfers between devices, shards(): grad_normed2 = lax.psum(column_back_part, 'mp')  75 us
    reduce_scatter x1, waiting for transfers between devices, shards(): lax.psum_scatter(qkv_weight_grad, 'dp', scatter_dimension=0, tiled=True)  72.9 us
    reduce_scatter x1, waiting for transfers between devices, shards(): lax.psum_scatter(up_weight_grad, 'dp', scatter_dimension=0, tiled=True)  72.9 us
    unnamed x1, blocking collectives  37.9 us
    unnamed x117, local copies, waits for them, and re-layouts  20.4 us
    reduce_scatter x1, waiting for transfers between devices, shards(): lax.psum_scatter(down_weight_grad, 'dp', scatter_dimension=1, tiled=True)  16.4 us
  transfers between devices with their start and end apart: 7, of which 7 were waited for; matrix products, arithmetic and copies ran while one was open for 13% of the time, Pallas kernels for 0%

commit v1 on v0

--- a/solution.py
+++ b/solution.py
@@ -120,7 +120,7 @@
     activated, gelu_pull = jax.vjp(exact_gelu, hidden_pre)
     hidden = activated.astype(jnp.bfloat16)
     column_part = jnp.dot(hidden, down_weight, preferred_element_type=jnp.float32)
-    fed = lax.psum(column_part, "mp")
+    fed = jnp.sum(lax.all_gather(column_part, "mp"), axis=0)
     layer_output = (middle + fed + down_bias.astype(jnp.float32)).astype(jnp.bfloat16)
     grad_out = cotangent.astype(jnp.float32)
     down_bias_grad = jnp.sum(grad_out, axis=0)

time: 756 us -> 810 us (1.071)
  waiting for transfers between devices: 500 us -> 544 us
  other arithmetic: 48.3 us -> 59.6 us
    all_gather x0 -> x1, waiting for transfers between devices: none -> 116 us  [shards(): fed = jnp.sum(lax.all_gather(column_part, 'mp'), axis=0)]
    psum x1, waiting for transfers between devices: 170 us -> 93.6 us  [shards(): grad_normed1 = lax.psum(head_back_part, 'mp')]
    reduce_sum x0 -> x1, other arithmetic: none -> 10.5 us  [shards(): fed = jnp.sum(lax.all_gather(column_part, 'mp'), axis=0)]
    unnamed x117 -> x105, local copies, waits for them, and re-layouts: 20.4 us -> 18.5 us
  transfers between devices with their start and end apart: 7 -> 8, of which waited for: 7 -> 8; matrix products, arithmetic and copies ran while one was open for 13% -> 13% of each run, Pallas kernels for 0% -> 0%
where the time goes in v1:
time: 810 us; the launch traced here: 803 us
  waiting for transfers between devices  544 us (67%)
  matrix products  93.4 us (12%)
  other arithmetic  59.6 us (7%)
  local copies, waits for them, and re-layouts  49.9 us (6%)
  blocking collectives  38.1 us (5%)
  between operations  16.2 us (2%)
    all_gather x1, waiting for transfers between devices, shards(): fed = jnp.sum(lax.all_gather(column_part, 'mp'), axis=0)  116 us
    psum x1, waiting for transfers between devices, shards(): grad_normed1 = lax.psum(head_back_part, 'mp')  93.6 us
    psum x1, waiting for transfers between devices, shards(): attended = lax.psum(head_part, 'mp')  87.3 us
    psum x1, waiting for transfers between devices, shards(): grad_normed2 = lax.psum(column_back_part, 'mp')  75 us
    reduce_scatter x1, waiting for transfers between devices, shards(): lax.psum_scatter(qkv_weight_grad, 'dp', scatter_dimension=0, tiled=True)  73.1 us
    reduce_scatter x1, waiting for transfers between devices, shards(): lax.psum_scatter(up_weight_grad, 'dp', scatter_dimension=0, tiled=True)  72.8 us
    unnamed x1, blocking collectives  38.1 us
    reduce_scatter x1, waiting for transfers between devices, shards(): lax.psum_scatter(down_weight_grad, 'dp', scatter_dimension=1, tiled=True)  20.4 us
  transfers between devices with their start and end apart: 8, of which 8 were waited for; matrix products, arithmetic and copies ran while one was open for 13% of the time, Pallas kernels for 0%

profile of v1, /device:TPU:0, one launch (start us, length us, event | category | flops | bytes accessed | tf_op | source)
XLA Modules:
  0.0 802.9 jit_solution(756818185542359470)
XLA Ops:
  19.8 5.2 reshape.266
  24.9 3.4 copy.53
  28.3 15.6 %while.22 = (s32[]{:T(128)}, bf16[3,512,3,64]{1,3,2,0:T(8,128)(2,1)}, f32[3,3,512,1]{2,1,3,0:T(4,128)}, bf16[3,512,3,3,64]{1,4,3,2,0:T(8,128)(2,1)}, s32[3,512]{1,0:T(4,128)S(1)}, /*index=5*/s32[]{:T(128)}) while((s32[]{:T(128)}, bf16[3,512,3,64]{1,3,2,0:T(8,128)(2,1)}, f32[3,3,512,1]{2,1,3,0:T(4,128)}, bf16[3,512,3,3,64]{1,4,3,2,0:T(8,128)(2,1)}, ...), condition=%wide.region_5.6_spmd, body=%wide.region_2.5_spmd.sunk | while | flops 211122688 | bytes 12513373 | solution.py:111
  46.5 4.0 fusion.76
  53.8 6.4 fusion.78
  60.2 87.3 %all-reduce.13.cloned.1.call-done = f32[1536,768]{1,0:T(8,128)} async-done(((f32[1536,768]{1,0:T(8,128)}), f32[1536,768]{1,0:T(8,128)}) %all-reduce.13.cloned.1.call-update) | async-done | bytes 4718608 | tf_op jit(solution)/shard_map/psum | solution.py:114
  147.5 3.1 fusion.74
  154.5 14.3 %convert_reduce_fusion.2 = (f32[768]{0:T(1024)}, bf16[1536,768]{1,0:T(8,128)(2,1)S(1)}) fusion(f32[1536,768]{1,0:T(8,128)S(1)} %bitcast.167, f32[768]{0:T(1024)S(1)} %copy-done.33, bf16[1536,768]{1,0:T(8,128)(2,1)S(1)} %add_convert_fusion.1, bf16[768,768]{1,0:T(8,128)(2,1)S(1)} %copy-done), kind=kOutput, calls=%fused_computation.78 | convolution fusion | flops 1900412160 | bytes 10622976 | tf_op jit(solution)/shard_map/dot_general | solution.py:134
  170.2 4.3 fusion.79
  174.6 12.9 %fusion.46 = bf16[1536,768]{1,0:T(8,128)(2,1)S(1)} fusion(bf16[1536,768]{1,0:T(8,128)(2,1)S(1)} %add_convert_fusion.1, bf16[768,768]{1,0:T(8,128)(2,1)S(1)} %copy-done, f32[768]{0:T(1024)} %reshape.274), kind=kOutput, calls=%fused_computation.72 | convolution fusion | flops 1889796096 | bytes 5901312 | tf_op jit(solution)/shard_map/dot_general | solution.py:119
  189.0 4.3 fusion.77
  193.9 75.0 %all-reduce.15.cloned.1.call-done = f32[1536,768]{1,0:T(8,128)} async-done(((f32[1536,768]{1,0:T(8,128)}), f32[1536,768]{1,0:T(8,128)}) %all-reduce.15.cloned.1.call-update) | async-done | bytes 4718608 | tf_op jit(solution)/shard_map/psum | solution.py:145
  268.8 5.4 multiply_reduce_fusion.1
  274.3 116.3 %all-gather.3.cloned.1.call-done = f32[6144,768]{1,0:T(8,128)} async-done(((f32[1536,768]{1,0:T(8,128)}), f32[6144,768]{1,0:T(8,128)}) %all-gather.3.cloned.1.call-update) | async-done | bytes 18874384 | tf_op jit(solution)/shard_map/all_gather | solution.py:123
  390.6 10.5 %reduce_sum.184 = f32[1536,768]{1,0:T(8,128)} reduce(f32[4,1536,768]{2,1,0:T(8,128)} %bitcast.157, f32[]{:T(128)} %constant.63.clone.1), dimensions={0}, to_apply=%region_9.10 | reduce | flops 3538944 | bytes 23592964 | tf_op jit(solution)/shard_map/reduce_sum | solution.py:123
  401.2 8.0 fusion.73
  413.2 3.4 convolution_convert_fusion
  417.5 21.1 %while.23 = (s32[]{:T(128)}, bf16[3,512,3,3,64]{1,4,3,2,0:T(8,128)(2,1)S(1)}, bf16[3,512,3,3,64]{1,4,3,2,0:T(8,128)(2,1)}, s32[3,512]{1,0:T(4,128)}, f32[3,3,512...) while((s32[]{:T(128)}, bf16[3,512,3,3,64]{1,4,3,2,0:T(8,128)(2,1)S(1)}, ...), condition=%wide.region_15.16_spmd, body=%wide.region_13.15_spmd.sunk | while | flops 512915968 | bytes 28481644 | solution.py:158
  439.8 3.1 copy.57
  442.9 3.8 reshape.270
  446.6 5.8 convolution_bitcast_fusion
  454.1 5.1 fusion.81
  459.5 6.0 fusion.80
  465.7 5.4 fusion.66
  474.9 5.3 reduce-scatter.15.cloned.1.call-done
  481.8 93.6 %all-reduce.17.cloned.1.call-done = f32[1536,768]{1,0:T(8,128)} async-done(((f32[1536,768]{1,0:T(8,128)}), f32[1536,768]{1,0:T(8,128)}) %all-reduce.17.cloned.1.call-update) | async-done | bytes 4718608 | tf_op jit(solution)/shard_map/psum | solution.py:172
  575.4 4.6 fusion.41
  580.0 38.1 %all-reduce.8 = (f32[768]{0:T(1024)S(1)}, f32[768]{0:T(1024)S(1)}, f32[2,3,64]{2,1,0:T(4,128)S(1)}, f32[768]{0:T(1024)S(1)}, f32[768]{0:T(1024)S(1)}, /*index=5*...) all-reduce(f32[768]{0:T(1024)S(1)} %get-tuple-element.140, ...), channel_id=3, replica_groups=mesh['dp'=8,'mp'=4] {'dp'}, use_global_device_ids=true, to_apply=%region_20.21.clone | all-reduce | flops 5760 | bytes 46080
  623.8 5.7 fusion.40
  629.4 20.4 %reduce-scatter.13.cloned.1.call-done = f32[768,96]{0,1:T(8,128)} async-done(((f32[768,768]{0,1:T(8,128)}), f32[768,96]{0,1:T(8,128)}) %reduce-scatter.13.cloned.1.call-update) | async-done | bytes 294928 | tf_op jit(solution)/shard_map/reduce_scatter | solution.py:185
  649.9 72.8 %reduce-scatter.11.cloned.1.call-done = f32[96,768]{1,0:T(8,128)} async-done(((f32[768,768]{1,0:T(8,128)}), f32[96,768]{1,0:T(8,128)}) %reduce-scatter.11.cloned.1.call-update) | async-done | bytes 294928 | tf_op jit(solution)/shard_map/reduce_scatter | solution.py:187
  722.7 73.1 %reduce-scatter.9.cloned.1.call-done = f32[96,3,192]{2,0,1:T(8,128)} async-done(((f32[768,3,192]{2,0,1:T(8,128)}), f32[96,3,192]{2,0,1:T(8,128)}) %reduce-scatter.9.cloned.1.call-update) | async-done | bytes 221200 | tf_op jit(solution)/shard_map/reduce_scatter | solution.py:179
  (214 shorter events, 79.9 us)
Async XLA Ops:
  7.2 145.8 %copy-start = (bf16[768,768]{1,0:T(8,128)(2,1)S(1)}, bf16[768,768]{1,0:T(8,128)(2,1)}, u32[]{:S(2)}) copy-start(bf16[768,768]{1,0:T(8,128)(2,1)} %param.29) | copy-start | bytes 3538948
  7.2 9.3 %copy-start.4 = (bf16[1536,768]{1,0:T(8,128)(2,1)S(1)}, bf16[1536,768]{1,0:T(8,128)(2,1)}, u32[]{:S(2)}) copy-start(bf16[1536,768]{1,0:T(8,128)(2,1)} %param.19) | copy-start | bytes 7077892
  7.2 140.3 %all-reduce.13.cloned.1.call-start = ((), (), s32[]{:S(2)}) async-start(), calls=%async_computation.4 | async-start | bytes 9437184 | tf_op jit(solution)/shard_map/psum | solution.py:114
  8.1 10.2 %copy-start.22 = (f32[768]{0:T(1024)}, f32[768]{0:T(1024)S(1)}, u32[]{:S(2)}) copy-start(f32[768]{0:T(1024)S(1)} %convert_element_type.122) | copy-start | bytes 9220
  8.9 9.4 %copy-start.30 = (f32[768]{0:T(1024)}, f32[768]{0:T(1024)S(1)}, u32[]{:S(2)}) copy-start(f32[768]{0:T(1024)S(1)} %convert_element_type.123) | copy-start | bytes 9220
  43.9 6.6 copy-start.17
  50.6 218.3 %all-reduce.15.cloned.1.call-start = ((), (), s32[]{:S(2)}) async-start(), calls=%async_computation.5 | async-start | bytes 9437184 | tf_op jit(solution)/shard_map/psum | solution.py:145
  147.5 5.5 slice-start
  154.5 20.1 %copy-start.6 = (bf16[1536,768]{1,0:T(8,128)(2,1)}, bf16[1536,768]{1,0:T(8,128)(2,1)S(1)}, u32[]{:S(2)}) copy-start(bf16[1536,768]{1,0:T(8,128)(2,1)S(1)} %add_convert_fusion.1) | copy-start | bytes 7077892
  174.5 216.1 %all-gather.3.cloned.1.call-start = ((), (), s32[]{:S(2)}) async-start(), calls=%async_computation.10 | async-start | bytes 23592960 | tf_op jit(solution)/shard_map/all_gather | solution.py:123
  174.6 14.4 %copy-start.39 = (bf16[768,768]{1,0:T(8,128)(2,1)S(1)}, bf16[768,768]{1,0:T(8,128)(2,1)}, u32[]{:S(2)}) copy-start(bf16[768,768]{1,0:T(8,128)(2,1)} %param.31) | copy-start | bytes 3538948
  193.2 75.6 %copy-start.21 = (f32[768]{0:T(1024)S(1)}, f32[768]{0:T(1024)}, u32[]{:S(2)}) copy-start(f32[768]{0:T(1024)} %convert_element_type.131) | copy-start | bytes 9220
  193.2 287.0 %reduce-scatter.15.cloned.1.call-start = ((), (), s32[]{:S(2)}) async-start(), calls=%async_computation.11 | async-start | bytes 884736
  390.6 10.5 %copy-start.9 = (bf16[1536,768]{1,0:T(8,128)(2,1)S(1)}, bf16[1536,768]{1,0:T(8,128)(2,1)}, u32[]{:S(2)}) copy-start(bf16[1536,768]{1,0:T(8,128)(2,1)} %param.33) | copy-start | bytes 7077892
  401.1 10.1 %copy-start.8 = (bf16[24,8,3,512]{3,1,2,0:T(8,128)(2,1)S(1)}, bf16[24,8,3,512]{3,1,2,0:T(8,128)(2,1)}, u32[]{:S(2)}) copy-start(bf16[24,8,3,512]{3,1,2,0:T(8,128)(2,1)} %copy-done.7) | copy-start | bytes 1769476
  416.7 158.7 %all-reduce.17.cloned.1.call-start = ((), (), s32[]{:S(2)}) async-start(), calls=%async_computation.6 | async-start | bytes 9437184 | tf_op jit(solution)/shard_map/psum | solution.py:172
  439.8 6.8 copy-start.41
  452.4 197.5 %reduce-scatter.13.cloned.1.call-start = ((), (), s32[]{:S(2)}) async-start(), calls=%async_computation.9 | async-start | bytes 2654208 | tf_op jit(solution)/shard_map/reduce_scatter | solution.py:185
  459.2 6.4 copy-start.5
  459.2 6.4 copy-start.16
  459.2 6.4 copy-start.19
  459.3 6.4 copy-start.23
  459.3 6.4 copy-start.31
  459.3 263.4 %reduce-scatter.11.cloned.1.call-start = ((), (), s32[]{:S(2)}) async-start(), calls=%async_computation.8 | async-start | bytes 2654208 | tf_op jit(solution)/shard_map/reduce_scatter | solution.py:187
  465.6 5.6 copy-start.42
  465.6 7.5 copy-start.29
  465.6 330.2 %reduce-scatter.9.cloned.1.call-start = ((), (), s32[]{:S(2)}) async-start(), calls=%async_computation.7 | async-start | bytes 2654208 | tf_op jit(solution)/shard_map/reduce_scatter | solution.py:179
  471.2 108.8 %copy-start.24 = (f32[768]{0:T(1024)S(1)}, f32[768]{0:T(1024)}, u32[]{:S(2)}) copy-start(f32[768]{0:T(1024)} %get-tuple-element.138) | copy-start | bytes 9220
  471.2 108.8 %copy-start.25 = (f32[768]{0:T(1024)S(1)}, f32[768]{0:T(1024)}, u32[]{:S(2)}) copy-start(f32[768]{0:T(1024)} %get-tuple-element.144) | copy-start | bytes 9220
  471.2 108.8 %copy-start.26 = (f32[768]{0:T(1024)S(1)}, f32[768]{0:T(1024)}, u32[]{:S(2)}) copy-start(f32[768]{0:T(1024)} %get-tuple-element.180) | copy-start | bytes 9220
  471.2 108.7 %copy-start.27 = (f32[768]{0:T(1024)S(1)}, f32[768]{0:T(1024)}, u32[]{:S(2)}) copy-start(f32[768]{0:T(1024)} %get-tuple-element.189) | copy-start | bytes 9220
  623.0 172.8 %copy-start.1 = (bf16[768,768]{1,0:T(8,128)(2,1)S(1)}, bf16[768,768]{1,0:T(8,128)(2,1)}, u32[]{:S(2)}) copy-start(bf16[768,768]{1,0:T(8,128)(2,1)} %param.29) | copy-start | bytes 3538948
  (22 other events, 53.5 us)
Sparse Core Ops, SparseCore 0:
  50.7 96.7 all-reduce.12
  174.6 94.1 all-reduce.14
  270.4 120.1 all-gather.2
  416.8 63.3 reduce-scatter.14
  482.4 92.9 all-reduce.16
  579.3 70.5 reduce-scatter.12
  653.9 68.6 reduce-scatter.10
  726.7 69.0 reduce-scatter.8
